TPU v7x, 32 devices: a whole 2x2x4 slice. The times are simulated.
32 devices in a mesh: member: 2 (over x), gx: 16 (over z, y, core).
Axes of the slice: x: 2, y: 2, z: 4, core: 2. Of those that a mesh axis runs over, the one named last changes fastest.
Arguments:
- spectrum: float32 [36, 32, 256, 128], P(None, None, ('member', 'gx')), parts along dimension 2, may hold values from 0 to 1
- wind: float32 [2, 256, 128], P(None, ('member', 'gx')), parts along dimension 1, may hold values from -32 to 32
- land_sea: int32 [128, 128], P('gx'), may hold values 0 or 1
- band_rows: int32 [128], replicated, may hold values from 0 to 127, each once
Outputs:
- spectrum_next: float32 [36, 32, 256, 128], P(None, None, ('member', 'gx')), parts along dimension 2
- ocean_fields: float32 [4, 128, 256], P(None, 'gx', 'member'), parts along dimension 2
There are 2 independent parts, one for each index of `member`. A program takes and returns all parts, laid end to end along the dimension named above; an argument that names none is the same for every part. Nothing has to cross between parts.
Inputs may be any that keep to these rules, and one draw needn't show every extreme that they name: band_rows names each of the 128 latitude rows exactly once.
All inputs are finite; a program needn't handle non-finite values. No bound on the sum of `land_sea` on one device may be relied on, other than what follows from the above.
Results may differ from a plain program's by a relative error of at most 0.00015.
Values sent between devices are 32-bit elements; how exact they have to be, the bound alone decides.
A program may use at most 128 MiB of HBM per device.

v0:
```python
import math
import jax
import jax.numpy as jnp
from jax import lax
from jax.sharding import PartitionSpec as P

STEPS = 3


def passed_along(value, axis, steps):
    count = lax.axis_size(axis)
    pairs = [(source, (source + steps) % count) for source in range(count)]
    return lax.ppermute(value, axis, pairs)


def wave_tables(directions, frequencies):
    angles = (jnp.arange(directions, dtype=jnp.float32) + 0.5) * (2.0 * math.pi / directions)
    levels = jnp.arange(frequencies, dtype=jnp.float32)
    shrink = jnp.power(jnp.float32(1.1), -levels)
    frequency = 0.0418 / shrink
    inverse_speed = 2.0 * math.pi * frequency / 9.81
    weight = (levels + 1.0) / frequencies
    cosine_dir = jnp.cos(angles)[:, None]
    sine_dir = jnp.sin(angles)[:, None]
    courant_x = 0.45 * shrink[None, :] * cosine_dir
    courant_y = 0.45 * shrink[None, :] * sine_dir
    factor = 3.0 / math.sqrt(directions * frequencies)
    project = jnp.stack(
        [factor * weight[None, :] * cosine_dir, factor * weight[None, :] * sine_dir]
    )
    return (courant_x, courant_y, cosine_dir, sine_dir, inverse_speed, weight * weight, project)


def upwind(center, west_cell, east_cell, courant_x, courant_y):
    along_x = courant_x[:, :, None, None]
    along_y = courant_y[:, :, None, None]
    border = jnp.zeros_like(center[..., :1])
    south_cell = jnp.concatenate([border, center[..., :-1]], axis=3)
    north_cell = jnp.concatenate([center[..., 1:], border], axis=3)
    return (
        center
        - jnp.maximum(along_x, 0.0) * (center - west_cell)
        + jnp.maximum(-along_x, 0.0) * (east_cell - center)
        - jnp.maximum(along_y, 0.0) * (center - south_cell)
        + jnp.maximum(-along_y, 0.0) * (north_cell - center)
    )


def sources(advected, wind_east, wind_north, sea_mask, tables):
    cosine_dir, sine_dir, inverse_speed, weight_two = (tables[2], tables[3], tables[4], tables[5])
    advected = advected * sea_mask
    energy = jnp.mean(advected, axis=(0, 1))
    wind_ratio = (
        wind_east * cosine_dir[:, :, None, None] + wind_north * sine_dir[:, :, None, None]
    ) * inverse_speed[None, :, None, None]
    growth = 0.05 * jnp.clip(wind_ratio - 1.0, 0.0, 4.0)
    damping = 0.3 * weight_two[None, :, None, None] * (energy / (0.5 + energy))
    return (advected * (1.0 + growth) / (1.0 + damping), growth * advected)


def coupling_fields(input_flux, current, project):
    stress = jnp.einsum("cij,ijxy->cxy", project, input_flux, precision=lax.Precision.HIGHEST)
    stokes = jnp.einsum("cij,ijxy->cxy", project, current, precision=lax.Precision.HIGHEST)
    return jnp.concatenate([stress, stokes], axis=0)


def per_device(spectrum, wind, land_sea, band_rows):
    tables = wave_tables(spectrum.shape[0], spectrum.shape[1])
    sea_mask = land_sea.astype(jnp.float32)
    current = spectrum
    quarter = spectrum.shape[0] // 4
    east_x = jnp.concatenate([tables[0][:quarter], tables[0][3 * quarter :]], axis=0)
    east_y = jnp.concatenate([tables[1][:quarter], tables[1][3 * quarter :]], axis=0)
    west_x = tables[0][quarter : 3 * quarter]
    west_y = tables[1][quarter : 3 * quarter]
    for step_index in range(STEPS):
        eastward = jnp.concatenate([current[:quarter], current[3 * quarter :]], axis=0)
        westward = current[quarter : 3 * quarter]
        from_west = passed_along(eastward[:, :, -1:], "gx", 1)
        from_east = passed_along(westward[:, :, :1], "gx", -1)
        west_cells = jnp.concatenate([from_west, eastward[:, :, :-1]], axis=2)
        east_cells = jnp.concatenate([westward[:, :, 1:], from_east], axis=2)
        moved_east = upwind(eastward, west_cells, eastward, east_x, east_y)
        moved_west = upwind(westward, westward, east_cells, west_x, west_y)
        advected = jnp.concatenate([moved_east[:quarter], moved_west, moved_east[quarter:]], axis=0)
        current, input_flux = sources(advected, wind[0], wind[1], sea_mask, tables)
    fields = coupling_fields(input_flux, current, tables[6])
    local_rows = jnp.transpose(fields[:, :, band_rows], (0, 2, 1))
    gathered = lax.all_gather(local_rows, "gx", axis=2, tiled=True)
    band_count = local_rows.shape[1] // lax.axis_size("gx")
    ocean_fields = lax.dynamic_slice_in_dim(
        gathered, lax.axis_index("gx") * band_count, band_count, 1
    )
    return (current, ocean_fields)


def solution(mesh):
    placed = (
        P(None, None, ("member", "gx"), None),
        P(None, ("member", "gx"), None),
        P("gx", None),
        P(),
    )
    return jax.shard_map(
        per_device,
        mesh=mesh,
        in_specs=placed,
        out_specs=(P(None, None, ("member", "gx"), None), P(None, "gx", "member")),
        check_vma=False,
    )
```

profile of v0, /device:TPU:0, one launch (start us, length us, event | category | flops | bytes accessed | tf_op | source)
XLA Modules:
  0.0 96.4 jit_solution(8376153678232764763)
XLA Ops:
  0.6 1.8 %fusion.60 = (f32[9,32,8,128]{3,2,1,0:T(8,128)S(1)}, f32[9,32,8,128]{3,2,1,0:T(8,128)S(1)}) fusion(f32[36,32,8,128]{3,2,1,0:T(8,128)} %param.4), kind=kLoop, calls=%fused_computation.121 | loop fusion | bytes 4718592 | tf_op jit(solution)/shard_map/slice | solution.py:77
  4.1 0.8 copy-done
  5.1 5.5 %collective-permute-start.1 = (f32[18,32,1,128]{3,1,2,0:T(8,128)S(1)}, f32[18,32,1,128]{3,1,2,0:T(8,128)S(1)}, u32[]{:S(2)}, u32[]{:S(2)}) collective-permute-start(f32[18,32,1,128]{3,1,2,0:T(8,128)S(1)} %bitcast.18), channel_id=1, source_target_pairs={{0,15},{1,0},{2,1},{3,2},{4,3},{5,4},{6,5},{7,6},{8,7},{9,8},{10,9... | collective-permute-start | bytes 884744 | tf_op jit(solution)/shard_map/ppermute | solution.py:13
  10.6 3.1 %fusion.64 = (f32[18,32,8,127]{3,1,2,0:T(8,128)}, f32[18,32,8,127]{3,1,2,0:T(8,128)}) fusion(f32[18,32,8,128]{3,1,2,0:T(8,128)S(1)} %copy_dynamic-update-slice_fusion), kind=kLoop, calls=%fused_computation.125 | loop fusion | bytes 9363456 | tf_op jit(solution)/shard_map/slice | solution.py:38
  13.7 1.6 %slice.229 = f32[18,32,7,128]{3,1,2,0:T(8,128)} slice(f32[18,32,8,128]{3,1,2,0:T(8,128)S(1)} %copy_dynamic-update-slice_fusion), slice={[0:18], [0:32], [0:7], [0:128]} | slice | bytes 4128768 | tf_op jit(solution)/shard_map/slice | solution.py:81
  15.5 0.8 fusion.59
  16.6 1.8 %copy.58 = f32[18,32,8,127]{3,1,2,0:T(8,128)} copy(f32[18,32,8,127]{3,2,1,0:T(8,128)S(1)} %get-tuple-element.20) | data formatting | bytes 4681728
  18.5 1.9 %copy.59 = f32[18,32,8,127]{3,1,2,0:T(8,128)} copy(f32[18,32,8,127]{3,2,1,0:T(8,128)S(1)} %get-tuple-element.21) | data formatting | bytes 4681728
  20.3 1.7 %copy.56 = f32[18,32,7,128]{3,1,2,0:T(8,128)} copy(f32[18,32,7,128]{3,2,1,0:T(8,128)S(1)} %slice.190) | data formatting | bytes 4128768
  22.4 4.0 %fusion.16 = f32[18,32,8,128]{3,1,2,0:T(8,128)S(1)} fusion(f32[18,32,8,128]{3,1,2,0:T(8,128)S(1)} %copy_dynamic-update-slice_fusion, f32[18,32,7,128]{3,1,2,0:T(8,128)} %slice.229, f32[18,32,1,128]{3,1,2,0:T(8,128)S(1)} %collective-permute-done, f32[18,32,8,127]{3,1,2,0:T(8,128)} %get-tuple-element.35, f32[18,32,8,127]{3,1,2,0:T(8,128)} %get-tuple-element.34, ...), kind=kLoop, calls=%fused_computation.43 | loop fusion | flops 7667712 | bytes 11768832 | tf_op jit(solution)/shard_map/add | solution.py:41
  26.7 1.4 %slice-done = f32[18,32,8,128]{3,2,1,0:T(8,128)S(1)} async-done(((f32[36,32,8,128]{3,2,1,0:T(8,128)}), f32[18,32,8,128]{3,2,1,0:T(8,128)S(1)}, s32[]{:S(2)}) %slice-start) | async-done | bytes 2359320 | tf_op jit(solution)/shard_map/slice | solution.py:78
  28.8 1.7 %fusion.20 = f32[18,32,8,128]{3,1,2,0:T(8,128)S(1)} fusion(f32[18,32,1,128]{3,1,2,0:T(8,128)S(1)} %collective-permute-done.1, f32[18,32,7,128]{3,1,2,0:T(8,128)S(1)} %copy-done.3, f32[18,32,8,127]{3,1,2,0:T(8,128)S(1)} %copy-done.2, f32[18,32,8,127]{3,1,2,0:T(8,128)S(1)} %copy-done.1, f32[18,32,8,128]{3,2,1,0:T(8,128)S(1)} %slice-done, ...), kind=kLoop, calls=%fused_computation.48 | loop fusion | flops 7667712 | bytes 11768832 | tf_op jit(solution)/shard_map/add | solution.py:41
  31.2 1.4 %multiply_divide_fusion.2 = f32[36,32,8,128]{3,1,2,0:T(8,128)S(1)} fusion(f32[9,32,8,128]{3,1,2,0:T(8,128)S(1)} %get-tuple-element.33, f32[18,32,8,128]{3,1,2,0:T(8,128)S(1)} %fusion.20, f32[9,32,8,128]{3,1,2,0:T(8,128)S(1)} %get-tuple-element.32, f32[32,8,128]{2,0,1:T(8,128)S(1)} %multiply_add_fusion.3, f32[32]{0:T(128)S(1)} %power_multiply_fusion, ...), kind=kLoop, calls=%fused_computation.10 | loop fusion | flops 11796480 | bytes 9719936 | tf_op jit(solution)/shard_map/div | solution.py:58
  32.6 0.9 fusion.57
  34.4 4.7 %collective-permute-start.3 = (f32[18,32,1,128]{3,1,2,0:T(8,128)S(1)}, f32[18,32,1,128]{3,1,2,0:T(8,128)S(1)}, u32[]{:S(2)}, u32[]{:S(2)}) collective-permute-start(f32[18,32,1,128]{3,1,2,0:T(8,128)S(1)} %slice.251), channel_id=1, source_target_pairs={{0,15},{1,0},{2,1},{3,2},{4,3},{5,4},{6,5},{7,6},{8,7},{9,8},{10,9... | collective-permute-start | bytes 884744 | tf_op jit(solution)/shard_map/ppermute | solution.py:13
  39.1 0.9 fusion.10
  39.9 2.8 %collective-permute-done.2 = f32[18,32,1,128]{3,1,2,0:T(8,128)S(1)} collective-permute-done((f32[18,32,1,128]{3,1,2,0:T(8,128)S(1)}, f32[18,32,1,128]{3,1,2,0:T(8,128)S(1)}, u32[]{:S(2)}, u32[]{:S(2)}) %collective-permute-start.2) | collective-permute-done | bytes 294944 | tf_op jit(solution)/shard_map/ppermute | solution.py:13
  42.7 1.9 %fusion.25 = f32[18,32,8,128]{3,1,2,0:T(8,128)S(1)} fusion(f32[18,32,7,128]{3,1,2,0:T(8,128)S(1)} %fusion.40, f32[18,32,1,128]{3,1,2,0:T(8,128)S(1)} %collective-permute-done.2, f32[18,32,8,127]{3,1,2,0:T(8,128)S(1)} %get-tuple-element.31, f32[18,32,8,127]{3,1,2,0:T(8,128)S(1)} %get-tuple-element.30, f32[9,32,8,128]{3,1,2,0:T(8,128)S(1)} %get-tuple-element.18, ...), kind=kLoop, calls=%fused_computation.54 | loop fusion | flops 8257536 | bytes 11768832 | tf_op jit(solution)/shard_map/add | solution.py:41
  44.9 1.8 %fusion.29 = f32[18,32,8,128]{3,1,2,0:T(8,128)S(1)} fusion(f32[18,32,1,128]{3,1,2,0:T(8,128)S(1)} %collective-permute-done.3, f32[18,32,7,128]{3,1,2,0:T(8,128)S(1)} %slice.250, f32[18,32,8,127]{3,1,2,0:T(8,128)S(1)} %get-tuple-element.17, f32[18,32,8,127]{3,1,2,0:T(8,128)S(1)} %get-tuple-element.16, f32[36,32,8,128]{3,1,2,0:T(8,128)S(1)} %multiply_divide_fusion.2, ...), kind=kLoop, calls=%fused_computation.59 | loop fusion | flops 7667712 | bytes 11768832 | tf_op jit(solution)/shard_map/add | solution.py:41
  47.4 1.4 %multiply_divide_fusion.1 = f32[36,32,8,128]{3,1,2,0:T(8,128)S(1)} fusion(f32[9,32,8,128]{3,1,2,0:T(8,128)S(1)} %get-tuple-element.29, f32[18,32,8,128]{3,1,2,0:T(8,128)S(1)} %fusion.29, f32[9,32,8,128]{3,1,2,0:T(8,128)S(1)} %get-tuple-element.28, f32[32,8,128]{2,0,1:T(8,128)S(1)} %multiply_add_fusion.2, f32[32]{0:T(128)S(1)} %power_multiply_fusion, ...), kind=kLoop, calls=%fused_computation.9 | loop fusion | flops 11796480 | bytes 9719936 | tf_op jit(solution)/shard_map/div | solution.py:58
  48.8 0.9 fusion.55
  50.5 4.5 %collective-permute-start.5 = (f32[18,32,1,128]{3,1,2,0:T(8,128)S(1)}, f32[18,32,1,128]{3,1,2,0:T(8,128)S(1)}, u32[]{:S(2)}, u32[]{:S(2)}) collective-permute-start(f32[18,32,1,128]{3,1,2,0:T(8,128)S(1)} %slice.268), channel_id=1, source_target_pairs={{0,15},{1,0},{2,1},{3,2},{4,3},{5,4},{6,5},{7,6},{8,7},{9,8},{10,9... | collective-permute-start | bytes 884744 | tf_op jit(solution)/shard_map/ppermute | solution.py:13
  55.0 0.9 fusion.8
  55.9 3.0 %collective-permute-done.4 = f32[18,32,1,128]{3,1,2,0:T(8,128)S(1)} collective-permute-done((f32[18,32,1,128]{3,1,2,0:T(8,128)S(1)}, f32[18,32,1,128]{3,1,2,0:T(8,128)S(1)}, u32[]{:S(2)}, u32[]{:S(2)}) %collective-permute-start.4) | collective-permute-done | bytes 294944 | tf_op jit(solution)/shard_map/ppermute | solution.py:13
  58.9 1.9 %fusion.34 = f32[18,32,8,128]{3,1,2,0:T(8,128)S(1)} fusion(f32[18,32,7,128]{3,1,2,0:T(8,128)S(1)} %fusion.39, f32[18,32,1,128]{3,1,2,0:T(8,128)S(1)} %collective-permute-done.4, f32[18,32,8,127]{3,1,2,0:T(8,128)S(1)} %get-tuple-element.27, f32[18,32,8,127]{3,1,2,0:T(8,128)S(1)} %get-tuple-element.26, f32[9,32,8,128]{3,1,2,0:T(8,128)S(1)} %get-tuple-element.14, ...), kind=kLoop, calls=%fused_computation.65 | loop fusion | flops 8257536 | bytes 11768832 | tf_op jit(solution)/shard_map/add | solution.py:41
  61.0 1.8 %fusion.38 = f32[18,32,8,128]{3,1,2,0:T(8,128)S(1)} fusion(f32[18,32,1,128]{3,1,2,0:T(8,128)S(1)} %collective-permute-done.5, f32[18,32,7,128]{3,1,2,0:T(8,128)S(1)} %slice.267, f32[18,32,8,127]{3,1,2,0:T(8,128)S(1)} %get-tuple-element.13, f32[18,32,8,127]{3,1,2,0:T(8,128)S(1)} %get-tuple-element.12, f32[36,32,8,128]{3,1,2,0:T(8,128)S(1)} %multiply_divide_fusion.1, ...), kind=kLoop, calls=%fused_computation.70 | loop fusion | flops 7667712 | bytes 11768832 | tf_op jit(solution)/shard_map/add | solution.py:41
  63.5 1.8 %fusion.4 = (f32[36,32,8,128]{3,1,2,0:T(8,128)S(1)}, f32[36,32,8,128]{3,1,2,0:T(8,128)S(1)}) fusion(f32[32]{0:T(128)S(1)} %power_multiply_fusion, f32[36,8,128]{2,1,0:T(8,128)S(1)} %multiply_add_fusion, f32[8,128]{1,0:T(8,128)S(1)} %convert_element_type.3, f32[9,32,8,128]{3,1,2,0:T(8,128)S(1)} %get-tuple-element.25, f32[18,32,8,128]{3,1,2,0:T(8,128)S(1)} %fusion.38, ...), kind=kLoop, calls=%fused_computation.12 | loop fusion | flops 12976128 | bytes 14438528 | tf_op jit(solution)/shard_map/mul | solution.py:58
  65.3 6.5 %copy.39 = f32[36,32,8,128]{3,2,1,0:T(8,128)} copy(f32[36,32,8,128]{3,1,2,0:T(8,128)S(1)} %get-tuple-element.11) | data formatting | bytes 9437184
  71.8 2.4 %fusion.45 = f32[2,8,128]{2,0,1:T(2,128)S(1)} fusion(f32[2,36,32,1]{2,0,1,3:T(2,128)S(1)} %copy.41, f32[36,32,8,128]{3,1,2,0:T(8,128)S(1)} %get-tuple-element.11), kind=kOutput, calls=%fused_computation.77 | convolution fusion | flops 28311552 | bytes 4736000 | tf_op jit(solution)/shard_map/cij,ijxy->cxy/dot_general | solution.py:63
  74.2 2.4 %fusion.42 = f32[2,8,128]{2,0,1:T(2,128)S(1)} fusion(f32[2,36,32,1]{2,0,1,3:T(2,128)S(1)} %copy.41, f32[36,32,8,128]{3,1,2,0:T(8,128)S(1)} %get-tuple-element.10), kind=kOutput, calls=%fused_computation.76 | convolution fusion | flops 28311552 | bytes 4736000 | tf_op jit(solution)/shard_map/cij,ijxy->cxy/dot_general | solution.py:62
  76.8 0.8 gather_fusion
  77.6 17.9 %all_gather.3 = f32[4,128,128]{1,0,2:T(4,128)S(1)} all-gather(f32[4,128,8]{1,0,2:T(4,128)S(1)} %copy.38), channel_id=1, replica_groups=mesh['member'=2,'gx'=16] {'gx'}, dimensions={2}, use_global_device_ids=true | all-gather | bytes 278528 | tf_op jit(solution)/shard_map/all_gather | solution.py:89
  (73 shorter events, 9.0 us)
Async XLA Ops:
  2.4 2.4 %copy-start = (f32[36,32,8,128]{3,2,1,0:T(8,128)S(1)}, f32[36,32,8,128]{3,2,1,0:T(8,128)}, u32[]{:S(2)}) copy-start(f32[36,32,8,128]{3,2,1,0:T(8,128)} %param.4) | copy-start | bytes 14155780
  3.6 18.8 %collective-permute-start = (f32[18,32,1,128]{3,1,2,0:T(8,128)}, f32[18,32,1,128]{3,1,2,0:T(8,128)S(1)}, u32[]{:S(2)}, u32[]{:S(2)}) collective-permute-start(f32[18,32,1,128]{3,1,2,0:T(8,128)} %slice.228), channel_id=1, source_target_pairs={{0,1},{1,2},{2,3},{3,4},{4,5},{5,6},{6,7},{7,8},{8,9},{9,10},{10,1... | collective-permute-start | bytes 884744 | tf_op jit(solution)/shard_map/ppermute | solution.py:13
  5.1 21.7 %collective-permute-start.1 = (f32[18,32,1,128]{3,1,2,0:T(8,128)S(1)}, f32[18,32,1,128]{3,1,2,0:T(8,128)S(1)}, u32[]{:S(2)}, u32[]{:S(2)}) collective-permute-start(f32[18,32,1,128]{3,1,2,0:T(8,128)S(1)} %bitcast.18), channel_id=1, source_target_pairs={{0,15},{1,0},{2,1},{3,2},{4,3},{5,4},{6,5},{7,6},{8,7},{9,8},{10,9... | collective-permute-start | bytes 884744 | tf_op jit(solution)/shard_map/ppermute | solution.py:13
  20.3 1.7 %copy-start.5 = (s32[8,128]{1,0:T(8,128)S(1)}, s32[8,128]{1,0:T(8,128)}, u32[]{:S(2)}) copy-start(s32[8,128]{1,0:T(8,128)} %param.6) | copy-start | bytes 12292
  20.3 1.7 %copy-start.4 = (f32[2,8,128]{2,1,0:T(8,128)S(1)}, f32[2,8,128]{2,1,0:T(8,128)}, u32[]{:S(2)}) copy-start(f32[2,8,128]{2,1,0:T(8,128)} %param.5) | copy-start | bytes 24580
  20.3 1.9 %copy-start.6 = (s32[128]{0:T(128)S(1)}, s32[128]{0:T(128)}, u32[]{:S(2)}) copy-start(s32[128]{0:T(128)} %param.7) | copy-start | bytes 1540
  22.4 4.3 %copy-start.2 = (f32[18,32,8,127]{3,1,2,0:T(8,128)S(1)}, f32[18,32,8,127]{3,1,2,0:T(8,128)}, u32[]{:S(2)}) copy-start(f32[18,32,8,127]{3,1,2,0:T(8,128)} %copy.59) | copy-start | bytes 7022596
  22.4 4.3 %copy-start.3 = (f32[18,32,7,128]{3,1,2,0:T(8,128)S(1)}, f32[18,32,7,128]{3,1,2,0:T(8,128)}, u32[]{:S(2)}) copy-start(f32[18,32,7,128]{3,1,2,0:T(8,128)} %copy.56) | copy-start | bytes 6193156
  26.4 1.7 %slice-start = ((f32[36,32,8,128]{3,2,1,0:T(8,128)}), f32[18,32,8,128]{3,2,1,0:T(8,128)S(1)}, s32[]{:S(2)}) async-start(f32[36,32,8,128]{3,2,1,0:T(8,128)} %param.4), calls=%async_computation | async-start | bytes 4718592 | tf_op jit(solution)/shard_map/slice | solution.py:78
  26.4 2.4 %copy-start.1 = (f32[18,32,8,127]{3,1,2,0:T(8,128)S(1)}, f32[18,32,8,127]{3,1,2,0:T(8,128)}, u32[]{:S(2)}) copy-start(f32[18,32,8,127]{3,1,2,0:T(8,128)} %copy.58) | copy-start | bytes 7022596
  33.8 8.9 %collective-permute-start.2 = (f32[18,32,1,128]{3,1,2,0:T(8,128)S(1)}, f32[18,32,1,128]{3,1,2,0:T(8,128)S(1)}, u32[]{:S(2)}, u32[]{:S(2)}) collective-permute-start(f32[18,32,1,128]{3,1,2,0:T(8,128)S(1)} %fusion.49), channel_id=1, source_target_pairs={{0,1},{1,2},{2,3},{3,4},{4,5},{5,6},{6,7},{7,8},{8,9},{9,10},{10,1... | collective-permute-start | bytes 884744 | tf_op jit(solution)/shard_map/ppermute | solution.py:13
  34.4 10.5 %collective-permute-start.3 = (f32[18,32,1,128]{3,1,2,0:T(8,128)S(1)}, f32[18,32,1,128]{3,1,2,0:T(8,128)S(1)}, u32[]{:S(2)}, u32[]{:S(2)}) collective-permute-start(f32[18,32,1,128]{3,1,2,0:T(8,128)S(1)} %slice.251), channel_id=1, source_target_pairs={{0,15},{1,0},{2,1},{3,2},{4,3},{5,4},{6,5},{7,6},{8,7},{9,8},{10,9... | collective-permute-start | bytes 884744 | tf_op jit(solution)/shard_map/ppermute | solution.py:13
  50.0 8.9 %collective-permute-start.4 = (f32[18,32,1,128]{3,1,2,0:T(8,128)S(1)}, f32[18,32,1,128]{3,1,2,0:T(8,128)S(1)}, u32[]{:S(2)}, u32[]{:S(2)}) collective-permute-start(f32[18,32,1,128]{3,1,2,0:T(8,128)S(1)} %fusion.48), channel_id=1, source_target_pairs={{0,1},{1,2},{2,3},{3,4},{4,5},{5,6},{6,7},{7,8},{8,9},{9,10},{10,1... | collective-permute-start | bytes 884744 | tf_op jit(solution)/shard_map/ppermute | solution.py:13
  50.5 10.5 %collective-permute-start.5 = (f32[18,32,1,128]{3,1,2,0:T(8,128)S(1)}, f32[18,32,1,128]{3,1,2,0:T(8,128)S(1)}, u32[]{:S(2)}, u32[]{:S(2)}) collective-permute-start(f32[18,32,1,128]{3,1,2,0:T(8,128)S(1)} %slice.268), channel_id=1, source_target_pairs={{0,15},{1,0},{2,1},{3,2},{4,3},{5,4},{6,5},{7,6},{8,7},{9,8},{10,9... | collective-permute-start | bytes 884744 | tf_op jit(solution)/shard_map/ppermute | solution.py:13
where the time goes:
time: 96.6 us; the launch traced here: 96.4 us
  local copies, waits for them, and re-layouts  29.2 us (30%)
  other arithmetic  22.3 us (23%)
  blocking collectives  17.9 us (19%)
  starting transfers between devices  15.3 us (16%)
  waiting for transfers between devices  5.77 us (6%)
  matrix products  4.79 us (5%)
  between operations  1.14 us (1%)
    all_gather x1, blocking collectives, per_device(): gathered = lax.all_gather(local_rows, 'gx', axis=2, tiled=True)  17.9 us
    ppermute x6, starting transfers between devices, passed_along(): return lax.ppermute(value, axis, pairs)  15.3 us
    unnamed x20, local copies, waits for them, and re-layouts  14.3 us
    add x6, other arithmetic, upwind(): center - jnp.maximum(along_x, 0.0) * (center - west_cell)  13.1 us
    ppermute x6, waiting for transfers between devices, passed_along(): return lax.ppermute(value, axis, pairs)  5.77 us
    slice x4, local copies, waits for them, and re-layouts, upwind(): south_cell = jnp.concatenate([border, center[..., :-1]], axis=3)  5.63 us
    div x2, other arithmetic, sources(): return (advected * (1.0 + growth) / (1.0 + damping), growth * advected)  2.77 us
    dot_general x1, matrix products, coupling_fields(): jnp.einsum('cij,ijxy->cxy', project, input_flux, precision=lax.Precision....  2.41 us
  transfers between devices with their start and end apart: 6, of which 2 were waited for; matrix products, arithmetic and copies ran while one was open for 24% of the time, Pallas kernels for 0%

commit v1 on v0

--- a/solution.py
+++ b/solution.py
@@ -86,7 +86,12 @@
         current, input_flux = sources(advected, wind[0], wind[1], sea_mask, tables)
     fields = coupling_fields(input_flux, current, tables[6])
     local_rows = jnp.transpose(fields[:, :, band_rows], (0, 2, 1))
-    gathered = lax.all_gather(local_rows, "gx", axis=2, tiled=True)
+    ring = [local_rows]
+    for hop in range(15):
+        ring.append(lax.ppermute(ring[-1], "gx", [(dev, (dev + 1) % 16) for dev in range(16)]))
+    gathered = jnp.roll(
+        jnp.concatenate(ring[::-1], axis=2), (lax.axis_index("gx") + 1) * ring[0].shape[2], axis=2
+    )
     band_count = local_rows.shape[1] // lax.axis_size("gx")
     ocean_fields = lax.dynamic_slice_in_dim(
         gathered, lax.axis_index("gx") * band_count, band_count, 1

time: 96.6 us -> 215 us (2.23)
  waiting for transfers between devices: 5.77 us -> 125 us
  blocking collectives: 17.9 us -> 0 us
  local copies, waits for them, and re-layouts: 29.2 us -> 46.8 us
    ppermute x0 -> x15, waiting for transfers between devices: none -> 119 us  [per_device(): lax.ppermute(ring[-1], 'gx', [(dev, (dev + 1) % 16) for dev in range(16)])]
    all_gather x1 -> x0, blocking collectives: 17.9 us -> none  [per_device(): gathered = lax.all_gather(local_rows, 'gx', axis=2, tiled=True)]
    concatenate x0 -> x1, local copies, waits for them, and re-layouts: none -> 14.1 us  [per_device(): jnp.roll(jnp.concatenate(ring[::-1], axis=2), (lax.axis_index('gx') + 1)...]
    unnamed x20 -> x24, local copies, waits for them, and re-layouts: 14.3 us -> 17.2 us
  transfers between devices with their start and end apart: 6 -> 21, of which waited for: 2 -> 16; matrix products, arithmetic and copies ran while one was open for 24% -> 15% of each run, Pallas kernels for 0% -> 0%
where the time goes in v1:
time: 215 us
  waiting for transfers between devices  125 us (58%)
  local copies, waits for them, and re-layouts  46.8 us (22%)
  other arithmetic  22.1 us (10%)
  starting transfers between devices  15.6 us (7%)
  matrix products  4.8 us (2%)
    ppermute x15, waiting for transfers between devices, per_device(): lax.ppermute(ring[-1], 'gx', [(dev, (dev + 1) % 16) for dev in range(16)])  119 us
    unnamed x24, local copies, waits for them, and re-layouts  17.2 us
    ppermute x6, starting transfers between devices, passed_along(): return lax.ppermute(value, axis, pairs)  15.5 us
    concatenate x1, local copies, waits for them, and re-layouts, per_device(): jnp.roll(jnp.concatenate(ring[::-1], axis=2), (lax.axis_index('gx') + 1)...  14.1 us
    add x6, other arithmetic, upwind(): center - jnp.maximum(along_x, 0.0) * (center - west_cell)  13.1 us
    slice x4, local copies, waits for them, and re-layouts, upwind(): south_cell = jnp.concatenate([border, center[..., :-1]], axis=3)  5.63 us
    ppermute x6, waiting for transfers between devices, passed_along(): return lax.ppermute(value, axis, pairs)  5.55 us
  transfers between devices with their start and end apart: 21, of which 16 were waited for; matrix products, arithmetic and copies ran while one was open for 15% of the time, Pallas kernels for 0%

profile of v1, /device:TPU:0, one launch (start us, length us, event | category | flops | bytes accessed | tf_op | source)
XLA Modules:
  0.0 215.0 jit_solution(11694411466555159869)
XLA Ops:
  0.6 1.8 fusion.60
  5.1 5.5 %collective-permute-start.1 = (f32[18,32,1,128]{3,1,2,0:T(8,128)S(1)}, f32[18,32,1,128]{3,1,2,0:T(8,128)S(1)}, u32[]{:S(2)}, u32[]{:S(2)}) collective-permute-start(f32[18,32,1,128]{3,1,2,0:T(8,128)S(1)} %bitcast.20), channel_id=1, source_target_pairs={{0,15},{1,0},{2,1},{3,2},{4,3},{5,4},{6,5},{7,6},{8,7},{9,8},{10,9... | collective-permute-start | bytes 884744 | tf_op jit(solution)/shard_map/ppermute | solution.py:13
  10.6 3.1 %fusion.64 = (f32[18,32,8,127]{3,1,2,0:T(8,128)}, f32[18,32,8,127]{3,1,2,0:T(8,128)}) fusion(f32[18,32,8,128]{3,1,2,0:T(8,128)S(1)} %copy_dynamic-update-slice_fusion), kind=kLoop, calls=%fused_computation.125 | loop fusion | bytes 9363456 | tf_op jit(solution)/shard_map/slice | solution.py:38
  16.6 1.8 copy.56
  18.5 1.8 copy.57
  22.4 4.0 %fusion.16 = f32[18,32,8,128]{3,1,2,0:T(8,128)S(1)} fusion(f32[18,32,8,128]{3,1,2,0:T(8,128)S(1)} %copy_dynamic-update-slice_fusion, f32[18,32,7,128]{3,1,2,0:T(8,128)} %slice.229, f32[18,32,1,128]{3,1,2,0:T(8,128)S(1)} %collective-permute-done, f32[18,32,8,127]{3,1,2,0:T(8,128)} %get-tuple-element.35, f32[18,32,8,127]{3,1,2,0:T(8,128)} %get-tuple-element.34, ...), kind=kLoop, calls=%fused_computation.43 | loop fusion | flops 7667712 | bytes 11768832 | tf_op jit(solution)/shard_map/add | solution.py:41
  34.4 4.7 %collective-permute-start.3 = (f32[18,32,1,128]{3,1,2,0:T(8,128)S(1)}, f32[18,32,1,128]{3,1,2,0:T(8,128)S(1)}, u32[]{:S(2)}, u32[]{:S(2)}) collective-permute-start(f32[18,32,1,128]{3,1,2,0:T(8,128)S(1)} %slice.251), channel_id=1, source_target_pairs={{0,15},{1,0},{2,1},{3,2},{4,3},{5,4},{6,5},{7,6},{8,7},{9,8},{10,9... | collective-permute-start | bytes 884744 | tf_op jit(solution)/shard_map/ppermute | solution.py:13
  39.9 2.8 %collective-permute-done.2 = f32[18,32,1,128]{3,1,2,0:T(8,128)S(1)} collective-permute-done((f32[18,32,1,128]{3,1,2,0:T(8,128)S(1)}, f32[18,32,1,128]{3,1,2,0:T(8,128)S(1)}, u32[]{:S(2)}, u32[]{:S(2)}) %collective-permute-start.2) | collective-permute-done | bytes 294944 | tf_op jit(solution)/shard_map/ppermute | solution.py:13
  42.7 1.9 fusion.25
  44.9 1.8 fusion.29
  50.5 4.7 %collective-permute-start.5 = (f32[18,32,1,128]{3,1,2,0:T(8,128)S(1)}, f32[18,32,1,128]{3,1,2,0:T(8,128)S(1)}, u32[]{:S(2)}, u32[]{:S(2)}) collective-permute-start(f32[18,32,1,128]{3,1,2,0:T(8,128)S(1)} %slice.268), channel_id=1, source_target_pairs={{0,15},{1,0},{2,1},{3,2},{4,3},{5,4},{6,5},{7,6},{8,7},{9,8},{10,9... | collective-permute-start | bytes 884744 | tf_op jit(solution)/shard_map/ppermute | solution.py:13
  56.1 2.8 %collective-permute-done.4 = f32[18,32,1,128]{3,1,2,0:T(8,128)S(1)} collective-permute-done((f32[18,32,1,128]{3,1,2,0:T(8,128)S(1)}, f32[18,32,1,128]{3,1,2,0:T(8,128)S(1)}, u32[]{:S(2)}, u32[]{:S(2)}) %collective-permute-start.4) | collective-permute-done | bytes 294944 | tf_op jit(solution)/shard_map/ppermute | solution.py:13
  58.8 1.9 fusion.34
  61.0 1.8 fusion.38
  65.0 2.4 %fusion.42 = f32[2,8,128]{2,0,1:T(2,128)S(1)} fusion(f32[2,36,32,1]{2,0,1,3:T(2,128)S(1)} %copy.39, f32[36,32,8,128]{3,1,2,0:T(8,128)S(1)} %get-tuple-element.10), kind=kOutput, calls=%fused_computation.76 | convolution fusion | flops 28311552 | bytes 4736000 | tf_op jit(solution)/shard_map/cij,ijxy->cxy/dot_general | solution.py:62
  67.4 2.4 %fusion.45 = f32[2,8,128]{2,0,1:T(2,128)S(1)} fusion(f32[2,36,32,1]{2,0,1,3:T(2,128)S(1)} %copy.39, f32[36,32,8,128]{3,1,2,0:T(8,128)S(1)} %get-tuple-element.11), kind=kOutput, calls=%fused_computation.77 | convolution fusion | flops 28311552 | bytes 4736000 | tf_op jit(solution)/shard_map/cij,ijxy->cxy/dot_general | solution.py:63
  70.9 8.5 %collective-permute-done.6 = f32[4,128,8]{2,0,1:T(4,128)S(1)} collective-permute-done((f32[4,128,8]{2,0,1:T(4,128)S(1)}, f32[4,128,8]{2,0,1:T(4,128)S(1)}, u32[]{:S(2)}, u32[]{:S(2)}) %collective-permute-start.6) | collective-permute-done | bytes 16416 | tf_op jit(solution)/shard_map/ppermute | solution.py:91
  79.3 8.5 %collective-permute-done.7 = f32[4,128,8]{2,0,1:T(4,128)S(1)} collective-permute-done((f32[4,128,8]{2,0,1:T(4,128)S(1)}, f32[4,128,8]{2,0,1:T(4,128)S(1)}, u32[]{:S(2)}, u32[]{:S(2)}) %collective-permute-start.7) | collective-permute-done | bytes 16416 | tf_op jit(solution)/shard_map/ppermute | solution.py:91
  87.8 8.5 %collective-permute-done.8 = f32[4,128,8]{2,0,1:T(4,128)S(1)} collective-permute-done((f32[4,128,8]{2,0,1:T(4,128)S(1)}, f32[4,128,8]{2,0,1:T(4,128)S(1)}, u32[]{:S(2)}, u32[]{:S(2)}) %collective-permute-start.8) | collective-permute-done | bytes 16416 | tf_op jit(solution)/shard_map/ppermute | solution.py:91
  96.3 8.5 %collective-permute-done.9 = f32[4,128,8]{2,0,1:T(4,128)S(1)} collective-permute-done((f32[4,128,8]{2,0,1:T(4,128)S(1)}, f32[4,128,8]{2,0,1:T(4,128)S(1)}, u32[]{:S(2)}, u32[]{:S(2)}) %collective-permute-start.9) | collective-permute-done | bytes 16416 | tf_op jit(solution)/shard_map/ppermute | solution.py:91
  104.8 8.5 %collective-permute-done.10 = f32[4,128,8]{2,0,1:T(4,128)S(1)} collective-permute-done((f32[4,128,8]{2,0,1:T(4,128)S(1)}, f32[4,128,8]{2,0,1:T(4,128)S(1)}, u32[]{:S(2)}, u32[]{:S(2)}) %collective-permute-start.10) | collective-permute-done | bytes 16416 | tf_op jit(solution)/shard_map/ppermute | solution.py:91
  113.3 8.5 %collective-permute-done.11 = f32[4,128,8]{2,0,1:T(4,128)S(1)} collective-permute-done((f32[4,128,8]{2,0,1:T(4,128)S(1)}, f32[4,128,8]{2,0,1:T(4,128)S(1)}, u32[]{:S(2)}, u32[]{:S(2)}) %collective-permute-start.11) | collective-permute-done | bytes 16416 | tf_op jit(solution)/shard_map/ppermute | solution.py:91
  121.8 8.5 %collective-permute-done.12 = f32[4,128,8]{2,0,1:T(4,128)S(1)} collective-permute-done((f32[4,128,8]{2,0,1:T(4,128)S(1)}, f32[4,128,8]{2,0,1:T(4,128)S(1)}, u32[]{:S(2)}, u32[]{:S(2)}) %collective-permute-start.12) | collective-permute-done | bytes 16416 | tf_op jit(solution)/shard_map/ppermute | solution.py:91
  130.3 8.5 %collective-permute-done.13 = f32[4,128,8]{2,0,1:T(4,128)S(1)} collective-permute-done((f32[4,128,8]{2,0,1:T(4,128)S(1)}, f32[4,128,8]{2,0,1:T(4,128)S(1)}, u32[]{:S(2)}, u32[]{:S(2)}) %collective-permute-start.13) | collective-permute-done | bytes 16416 | tf_op jit(solution)/shard_map/ppermute | solution.py:91
  138.8 8.5 %collective-permute-done.14 = f32[4,128,8]{2,0,1:T(4,128)S(1)} collective-permute-done((f32[4,128,8]{2,0,1:T(4,128)S(1)}, f32[4,128,8]{2,0,1:T(4,128)S(1)}, u32[]{:S(2)}, u32[]{:S(2)}) %collective-permute-start.14) | collective-permute-done | bytes 16416 | tf_op jit(solution)/shard_map/ppermute | solution.py:91
  147.3 8.5 %collective-permute-done.15 = f32[4,128,8]{2,0,1:T(4,128)S(1)} collective-permute-done((f32[4,128,8]{2,0,1:T(4,128)S(1)}, f32[4,128,8]{2,0,1:T(4,128)S(1)}, u32[]{:S(2)}, u32[]{:S(2)}) %collective-permute-start.15) | collective-permute-done | bytes 16416 | tf_op jit(solution)/shard_map/ppermute | solution.py:91
  155.8 8.5 %collective-permute-done.16 = f32[4,128,8]{2,0,1:T(4,128)S(1)} collective-permute-done((f32[4,128,8]{2,0,1:T(4,128)S(1)}, f32[4,128,8]{2,0,1:T(4,128)S(1)}, u32[]{:S(2)}, u32[]{:S(2)}) %collective-permute-start.16) | collective-permute-done | bytes 16416 | tf_op jit(solution)/shard_map/ppermute | solution.py:91
  164.3 8.5 %collective-permute-done.17 = f32[4,128,8]{2,0,1:T(4,128)S(1)} collective-permute-done((f32[4,128,8]{2,0,1:T(4,128)S(1)}, f32[4,128,8]{2,0,1:T(4,128)S(1)}, u32[]{:S(2)}, u32[]{:S(2)}) %collective-permute-start.17) | collective-permute-done | bytes 16416 | tf_op jit(solution)/shard_map/ppermute | solution.py:91
  172.8 8.5 %collective-permute-done.18 = f32[4,128,8]{2,0,1:T(4,128)S(1)} collective-permute-done((f32[4,128,8]{2,0,1:T(4,128)S(1)}, f32[4,128,8]{2,0,1:T(4,128)S(1)}, u32[]{:S(2)}, u32[]{:S(2)}) %collective-permute-start.18) | collective-permute-done | bytes 16416 | tf_op jit(solution)/shard_map/ppermute | solution.py:91
  182.0 8.6 %collective-permute-done.19 = f32[4,128,8]{2,0,1:T(4,128)} collective-permute-done((f32[4,128,8]{2,0,1:T(4,128)S(1)}, f32[4,128,8]{2,0,1:T(4,128)}, u32[]{:S(2)}, u32[]{:S(2)}) %collective-permute-start.19) | collective-permute-done | bytes 16416 | tf_op jit(solution)/shard_map/ppermute | solution.py:91
  190.6 8.9 %copy.37 = f32[36,32,8,128]{3,2,1,0:T(8,128)} copy(f32[36,32,8,128]{3,1,2,0:T(8,128)} %copy-done) | data formatting | bytes 9437184
  199.4 14.1 %concatenate.130 = f32[4,128,256]{2,0,1:T(4,128)} concatenate(f32[4,128,8]{2,0,1:T(4,128)} %collective-permute-done.20, f32[4,128,8]{2,0,1:T(4,128)} %collective-permute-done.19, f32[4,128,8]{2,0,1:T(4,128)} %copy-done.5, f32[4,128,8]{2,0,1:T(4,128)S(1)} %collective-permute-done.17, f32[4,128,8]{2,0,1:T(4,128)S(1)} %collective-permute-done.16, ...), dimensions={2} | concatenate | bytes 1048576 | tf_op jit(solution)/shard_map/jit(_roll_dynamic)/concatenate | solution.py:92
  (106 shorter events, 26.8 us)
Async XLA Ops:
  2.4 2.4 %copy-start.1 = (f32[36,32,8,128]{3,2,1,0:T(8,128)S(1)}, f32[36,32,8,128]{3,2,1,0:T(8,128)}, u32[]{:S(2)}) copy-start(f32[36,32,8,128]{3,2,1,0:T(8,128)} %param.4) | copy-start | bytes 14155780
  3.6 18.8 %collective-permute-start = (f32[18,32,1,128]{3,1,2,0:T(8,128)}, f32[18,32,1,128]{3,1,2,0:T(8,128)S(1)}, u32[]{:S(2)}, u32[]{:S(2)}) collective-permute-start(f32[18,32,1,128]{3,1,2,0:T(8,128)} %slice.228), channel_id=1, source_target_pairs={{0,1},{1,2},{2,3},{3,4},{4,5},{5,6},{6,7},{7,8},{8,9},{9,10},{10,1... | collective-permute-start | bytes 884744 | tf_op jit(solution)/shard_map/ppermute | solution.py:13
  5.1 21.7 %collective-permute-start.1 = (f32[18,32,1,128]{3,1,2,0:T(8,128)S(1)}, f32[18,32,1,128]{3,1,2,0:T(8,128)S(1)}, u32[]{:S(2)}, u32[]{:S(2)}) collective-permute-start(f32[18,32,1,128]{3,1,2,0:T(8,128)S(1)} %bitcast.20), channel_id=1, source_target_pairs={{0,15},{1,0},{2,1},{3,2},{4,3},{5,4},{6,5},{7,6},{8,7},{9,8},{10,9... | collective-permute-start | bytes 884744 | tf_op jit(solution)/shard_map/ppermute | solution.py:13
  20.3 1.7 copy-start.7
  20.3 1.7 copy-start.6
  20.3 1.9 copy-start.8
  22.4 4.3 %copy-start.3 = (f32[18,32,8,127]{3,1,2,0:T(8,128)S(1)}, f32[18,32,8,127]{3,1,2,0:T(8,128)}, u32[]{:S(2)}) copy-start(f32[18,32,8,127]{3,1,2,0:T(8,128)} %copy.57) | copy-start | bytes 7022596
  22.4 4.3 %copy-start.4 = (f32[18,32,7,128]{3,1,2,0:T(8,128)S(1)}, f32[18,32,7,128]{3,1,2,0:T(8,128)}, u32[]{:S(2)}) copy-start(f32[18,32,7,128]{3,1,2,0:T(8,128)} %copy.54) | copy-start | bytes 6193156
  26.4 1.7 slice-start
  26.4 2.4 %copy-start.2 = (f32[18,32,8,127]{3,1,2,0:T(8,128)S(1)}, f32[18,32,8,127]{3,1,2,0:T(8,128)}, u32[]{:S(2)}) copy-start(f32[18,32,8,127]{3,1,2,0:T(8,128)} %copy.56) | copy-start | bytes 7022596
  33.8 8.9 %collective-permute-start.2 = (f32[18,32,1,128]{3,1,2,0:T(8,128)S(1)}, f32[18,32,1,128]{3,1,2,0:T(8,128)S(1)}, u32[]{:S(2)}, u32[]{:S(2)}) collective-permute-start(f32[18,32,1,128]{3,1,2,0:T(8,128)S(1)} %fusion.49), channel_id=1, source_target_pairs={{0,1},{1,2},{2,3},{3,4},{4,5},{5,6},{6,7},{7,8},{8,9},{9,10},{10,1... | collective-permute-start | bytes 884744 | tf_op jit(solution)/shard_map/ppermute | solution.py:13
  34.4 10.5 %collective-permute-start.3 = (f32[18,32,1,128]{3,1,2,0:T(8,128)S(1)}, f32[18,32,1,128]{3,1,2,0:T(8,128)S(1)}, u32[]{:S(2)}, u32[]{:S(2)}) collective-permute-start(f32[18,32,1,128]{3,1,2,0:T(8,128)S(1)} %slice.251), channel_id=1, source_target_pairs={{0,15},{1,0},{2,1},{3,2},{4,3},{5,4},{6,5},{7,6},{8,7},{9,8},{10,9... | collective-permute-start | bytes 884744 | tf_op jit(solution)/shard_map/ppermute | solution.py:13
  49.9 8.9 %collective-permute-start.4 = (f32[18,32,1,128]{3,1,2,0:T(8,128)S(1)}, f32[18,32,1,128]{3,1,2,0:T(8,128)S(1)}, u32[]{:S(2)}, u32[]{:S(2)}) collective-permute-start(f32[18,32,1,128]{3,1,2,0:T(8,128)S(1)} %fusion.48), channel_id=1, source_target_pairs={{0,1},{1,2},{2,3},{3,4},{4,5},{5,6},{6,7},{7,8},{8,9},{9,10},{10,1... | collective-permute-start | bytes 884744 | tf_op jit(solution)/shard_map/ppermute | solution.py:13
  50.5 10.5 %collective-permute-start.5 = (f32[18,32,1,128]{3,1,2,0:T(8,128)S(1)}, f32[18,32,1,128]{3,1,2,0:T(8,128)S(1)}, u32[]{:S(2)}, u32[]{:S(2)}) collective-permute-start(f32[18,32,1,128]{3,1,2,0:T(8,128)S(1)} %slice.268), channel_id=1, source_target_pairs={{0,15},{1,0},{2,1},{3,2},{4,3},{5,4},{6,5},{7,6},{8,7},{9,8},{10,9... | collective-permute-start | bytes 884744 | tf_op jit(solution)/shard_map/ppermute | solution.py:13
  65.0 2.4 %copy-start = (f32[36,32,8,128]{3,1,2,0:T(8,128)}, f32[36,32,8,128]{3,1,2,0:T(8,128)S(1)}, u32[]{:S(2)}) copy-start(f32[36,32,8,128]{3,1,2,0:T(8,128)S(1)} %get-tuple-element.11) | copy-start | bytes 14155780
  70.8 8.5 %collective-permute-start.6 = (f32[4,128,8]{2,0,1:T(4,128)S(1)}, f32[4,128,8]{2,0,1:T(4,128)S(1)}, u32[]{:S(2)}, u32[]{:S(2)}) collective-permute-start(f32[4,128,8]{2,0,1:T(4,128)S(1)} %bitcast.17), channel_id=1, source_target_pairs={{0,1},{1,2},{2,3},{3,4},{4,5},{5,6},{6,7},{7,8},{8,9},{9,10},{10,1... | collective-permute-start | bytes 49160 | tf_op jit(solution)/shard_map/ppermute | solution.py:91
  79.3 8.5 %collective-permute-start.7 = (f32[4,128,8]{2,0,1:T(4,128)S(1)}, f32[4,128,8]{2,0,1:T(4,128)S(1)}, u32[]{:S(2)}, u32[]{:S(2)}) collective-permute-start(f32[4,128,8]{2,0,1:T(4,128)S(1)} %collective-permute-done.6), channel_id=1, source_target_pairs={{0,1},{1,2},{2,3},{3,4},{4,5},{5,6},{6,7},{7,8},{8,9},{9,10},{10,1... | collective-permute-start | bytes 49160 | tf_op jit(solution)/shard_map/ppermute | solution.py:91
  87.8 8.5 %collective-permute-start.8 = (f32[4,128,8]{2,0,1:T(4,128)S(1)}, f32[4,128,8]{2,0,1:T(4,128)S(1)}, u32[]{:S(2)}, u32[]{:S(2)}) collective-permute-start(f32[4,128,8]{2,0,1:T(4,128)S(1)} %collective-permute-done.7), channel_id=1, source_target_pairs={{0,1},{1,2},{2,3},{3,4},{4,5},{5,6},{6,7},{7,8},{8,9},{9,10},{10,1... | collective-permute-start | bytes 49160 | tf_op jit(solution)/shard_map/ppermute | solution.py:91
  96.3 8.5 %collective-permute-start.9 = (f32[4,128,8]{2,0,1:T(4,128)S(1)}, f32[4,128,8]{2,0,1:T(4,128)S(1)}, u32[]{:S(2)}, u32[]{:S(2)}) collective-permute-start(f32[4,128,8]{2,0,1:T(4,128)S(1)} %collective-permute-done.8), channel_id=1, source_target_pairs={{0,1},{1,2},{2,3},{3,4},{4,5},{5,6},{6,7},{7,8},{8,9},{9,10},{10,1... | collective-permute-start | bytes 49160 | tf_op jit(solution)/shard_map/ppermute | solution.py:91
  104.8 8.5 %collective-permute-start.10 = (f32[4,128,8]{2,0,1:T(4,128)S(1)}, f32[4,128,8]{2,0,1:T(4,128)S(1)}, u32[]{:S(2)}, u32[]{:S(2)}) collective-permute-start(f32[4,128,8]{2,0,1:T(4,128)S(1)} %collective-permute-done.9), channel_id=1, source_target_pairs={{0,1},{1,2},{2,3},{3,4},{4,5},{5,6},{6,7},{7,8},{8,9},{9,10},{10,1... | collective-permute-start | bytes 49160 | tf_op jit(solution)/shard_map/ppermute | solution.py:91
  113.3 8.5 %collective-permute-start.11 = (f32[4,128,8]{2,0,1:T(4,128)S(1)}, f32[4,128,8]{2,0,1:T(4,128)S(1)}, u32[]{:S(2)}, u32[]{:S(2)}) collective-permute-start(f32[4,128,8]{2,0,1:T(4,128)S(1)} %collective-permute-done.10), channel_id=1, source_target_pairs={{0,1},{1,2},{2,3},{3,4},{4,5},{5,6},{6,7},{7,8},{8,9},{9,10},{10,1... | collective-permute-start | bytes 49160 | tf_op jit(solution)/shard_map/ppermute | solution.py:91
  121.8 8.5 %collective-permute-start.12 = (f32[4,128,8]{2,0,1:T(4,128)S(1)}, f32[4,128,8]{2,0,1:T(4,128)S(1)}, u32[]{:S(2)}, u32[]{:S(2)}) collective-permute-start(f32[4,128,8]{2,0,1:T(4,128)S(1)} %collective-permute-done.11), channel_id=1, source_target_pairs={{0,1},{1,2},{2,3},{3,4},{4,5},{5,6},{6,7},{7,8},{8,9},{9,10},{10,1... | collective-permute-start | bytes 49160 | tf_op jit(solution)/shard_map/ppermute | solution.py:91
  130.3 8.5 %collective-permute-start.13 = (f32[4,128,8]{2,0,1:T(4,128)S(1)}, f32[4,128,8]{2,0,1:T(4,128)S(1)}, u32[]{:S(2)}, u32[]{:S(2)}) collective-permute-start(f32[4,128,8]{2,0,1:T(4,128)S(1)} %collective-permute-done.12), channel_id=1, source_target_pairs={{0,1},{1,2},{2,3},{3,4},{4,5},{5,6},{6,7},{7,8},{8,9},{9,10},{10,1... | collective-permute-start | bytes 49160 | tf_op jit(solution)/shard_map/ppermute | solution.py:91
  138.8 8.5 %collective-permute-start.14 = (f32[4,128,8]{2,0,1:T(4,128)S(1)}, f32[4,128,8]{2,0,1:T(4,128)S(1)}, u32[]{:S(2)}, u32[]{:S(2)}) collective-permute-start(f32[4,128,8]{2,0,1:T(4,128)S(1)} %collective-permute-done.13), channel_id=1, source_target_pairs={{0,1},{1,2},{2,3},{3,4},{4,5},{5,6},{6,7},{7,8},{8,9},{9,10},{10,1... | collective-permute-start | bytes 49160 | tf_op jit(solution)/shard_map/ppermute | solution.py:91
  147.3 8.5 %collective-permute-start.15 = (f32[4,128,8]{2,0,1:T(4,128)S(1)}, f32[4,128,8]{2,0,1:T(4,128)S(1)}, u32[]{:S(2)}, u32[]{:S(2)}) collective-permute-start(f32[4,128,8]{2,0,1:T(4,128)S(1)} %collective-permute-done.14), channel_id=1, source_target_pairs={{0,1},{1,2},{2,3},{3,4},{4,5},{5,6},{6,7},{7,8},{8,9},{9,10},{10,1... | collective-permute-start | bytes 49160 | tf_op jit(solution)/shard_map/ppermute | solution.py:91
  155.8 8.5 %collective-permute-start.16 = (f32[4,128,8]{2,0,1:T(4,128)S(1)}, f32[4,128,8]{2,0,1:T(4,128)S(1)}, u32[]{:S(2)}, u32[]{:S(2)}) collective-permute-start(f32[4,128,8]{2,0,1:T(4,128)S(1)} %collective-permute-done.15), channel_id=1, source_target_pairs={{0,1},{1,2},{2,3},{3,4},{4,5},{5,6},{6,7},{7,8},{8,9},{9,10},{10,1... | collective-permute-start | bytes 49160 | tf_op jit(solution)/shard_map/ppermute | solution.py:91
  164.3 8.5 %collective-permute-start.17 = (f32[4,128,8]{2,0,1:T(4,128)S(1)}, f32[4,128,8]{2,0,1:T(4,128)S(1)}, u32[]{:S(2)}, u32[]{:S(2)}) collective-permute-start(f32[4,128,8]{2,0,1:T(4,128)S(1)} %collective-permute-done.16), channel_id=1, source_target_pairs={{0,1},{1,2},{2,3},{3,4},{4,5},{5,6},{6,7},{7,8},{8,9},{9,10},{10,1... | collective-permute-start | bytes 49160 | tf_op jit(solution)/shard_map/ppermute | solution.py:91
  172.8 8.5 %collective-permute-start.18 = (f32[4,128,8]{2,0,1:T(4,128)S(1)}, f32[4,128,8]{2,0,1:T(4,128)S(1)}, u32[]{:S(2)}, u32[]{:S(2)}) collective-permute-start(f32[4,128,8]{2,0,1:T(4,128)S(1)} %collective-permute-done.17), channel_id=1, source_target_pairs={{0,1},{1,2},{2,3},{3,4},{4,5},{5,6},{6,7},{7,8},{8,9},{9,10},{10,1... | collective-permute-start | bytes 49160 | tf_op jit(solution)/shard_map/ppermute | solution.py:91
  181.3 0.7 copy-start.5
  182.0 8.6 %collective-permute-start.19 = (f32[4,128,8]{2,0,1:T(4,128)S(1)}, f32[4,128,8]{2,0,1:T(4,128)}, u32[]{:S(2)}, u32[]{:S(2)}) collective-permute-start(f32[4,128,8]{2,0,1:T(4,128)S(1)} %collective-permute-done.18), channel_id=1, source_target_pairs={{0,1},{1,2},{2,3},{3,4},{4,5},{5,6},{6,7},{7,8},{8,9},{9,10},{10,1... | collective-permute-start | bytes 49160 | tf_op jit(solution)/shard_map/ppermute | solution.py:91
  190.6 8.9 %collective-permute-start.20 = (f32[4,128,8]{2,0,1:T(4,128)}, f32[4,128,8]{2,0,1:T(4,128)}, u32[]{:S(2)}, u32[]{:S(2)}) collective-permute-start(f32[4,128,8]{2,0,1:T(4,128)} %collective-permute-done.19), channel_id=1, source_target_pairs={{0,1},{1,2},{2,3},{3,4},{4,5},{5,6},{6,7},{7,8},{8,9},{9,10},{10,1... | collective-permute-start | bytes 49160 | tf_op jit(solution)/shard_map/ppermute | solution.py:91
